TPU v7x, 32 devices: a whole 2x2x4 slice. The times are simulated.
32 devices in a mesh: dp: 8 (over z, x), rep: 4 (over y, core).
Axes of the slice: x: 2, y: 2, z: 4, core: 2. Of those that a mesh axis runs over, the one named last changes fastest.
Arguments:
- token_inputs: bfloat16 [16384, 2048], P(('dp', 'rep')), may hold values from -12 to 12
- cotangent: bfloat16 [16384, 2048], P(('dp', 'rep')), may hold values from -6 to 6
- gate_preact: bfloat16 [16384, 768], P(('dp', 'rep')), may hold values from -6 to 6
- up_preact: bfloat16 [16384, 768], P(('dp', 'rep')), may hold values from -6 to 6
- down_weight: bfloat16 [2, 768, 2048], P(None, None, 'dp'), may hold values from -0.21875 to 0.21875
- block_expert: int32 [128], P(('dp', 'rep')), may hold values from 0 to 1
- block_count: int32 [128], P(('dp', 'rep')), may hold values from 1 to 128, as said below
Outputs:
- update: bfloat16 [2, 3, 768, 2048], P(None, None, None, 'dp')
Inputs may be any that keep to these rules, and one draw needn't show every extreme that they name: `block_count`: live rows of a block, at most 128; in every draw some block is full.
All inputs are finite; a program needn't handle non-finite values.
Results may differ from a plain program's by a relative error of at most 0.02.
Values may be sent and summed in bfloat16 or wider, within the bound.
A program may use at most 128 MiB of HBM per device.

v0:
```python
import math
import jax
import jax.numpy as jnp
from jax import lax
from jax.sharding import PartitionSpec as P

D = 2048
ITERS = 2
ns_first = 3.4445
ns_second = -4.775
ns_third = 2.0315
norm_eps = 1e-07


def whole_sweeps(matrix, column_width, groups_all, sweeps, scale):
    hidden_width = matrix.shape[0]
    group = math.gcd(8, groups_all)
    current = matrix
    result = None
    for sweep in range(sweeps):

        def add_group(index, total):
            cols = lax.dynamic_slice_in_dim(
                current, index * group * column_width, group * column_width, 1
            )
            cols = cols.reshape(hidden_width, group, column_width)
            term = jnp.einsum(
                "fnd,gnd->nfg", cols, cols, preferred_element_type=jnp.float32
            ).astype(jnp.bfloat16)
            return total + jnp.sum(lax.optimization_barrier(term).astype(jnp.float32), axis=0)

        gram = lax.fori_loop(
            0, groups_all // group, add_group, jnp.zeros((hidden_width, hidden_width), jnp.float32)
        )
        gram_half = gram.astype(jnp.bfloat16)
        squared = jnp.dot(gram_half, gram_half, preferred_element_type=jnp.float32)
        poly = (ns_second * gram + ns_third * squared).astype(jnp.bfloat16)
        newer = ns_first * current.astype(jnp.float32) + jnp.dot(
            poly, current, preferred_element_type=jnp.float32
        )
        if sweep + 1 < sweeps:
            current = newer.astype(jnp.bfloat16)
        else:
            result = (scale * newer).astype(jnp.bfloat16)
    return result


def per_device(
    token_inputs, cotangent, gate_preact, up_preact, down_weight, block_expert, block_count
):
    blocks = block_count.shape[0]
    rows_here = token_inputs.shape[0]
    hidden_width = gate_preact.shape[1]
    width = token_inputs.shape[1]
    block_rows = rows_here // blocks
    experts_here = down_weight.shape[0]
    row_place = jnp.arange(rows_here, dtype=jnp.int32) % block_rows
    row_count = jnp.repeat(block_count, block_rows, total_repeat_length=rows_here)
    row_expert = jnp.repeat(block_expert, block_rows, total_repeat_length=rows_here)
    live_rows = row_place < row_count
    masked = jnp.where(live_rows[:, None], cotangent, jnp.zeros_like(cotangent))
    gate = gate_preact.astype(jnp.float32)
    upper = up_preact.astype(jnp.float32)
    sigmoid_gate = jax.nn.sigmoid(gate)
    hidden = (gate * sigmoid_gate * upper).astype(jnp.bfloat16)
    selector = (row_expert[None, :] == jnp.arange(experts_here, dtype=jnp.int32)[:, None]).astype(
        jnp.bfloat16
    )
    masked_each = masked[None, :, :] * selector[:, :, None]
    weights_all = lax.all_gather(down_weight, "dp", axis=2, tiled=True)
    back = jnp.einsum("erd,efd->rf", masked_each, weights_all, preferred_element_type=jnp.float32)
    grad_gate = (back * upper * sigmoid_gate * (1.0 + gate * (1.0 - sigmoid_gate))).astype(
        jnp.bfloat16
    )
    grad_up = (back * gate * sigmoid_gate).astype(jnp.bfloat16)
    gate_up = jnp.concatenate([grad_gate, grad_up], axis=1)
    gate_up_each = gate_up[None, :, :] * selector[:, :, None]
    hidden_each = hidden[None, :, :] * selector[:, :, None]
    input_part = jnp.einsum(
        "erf,rd->efd", gate_up_each, token_inputs, preferred_element_type=jnp.float32
    )
    output_part = jnp.einsum("erf,rd->efd", hidden_each, masked, preferred_element_type=jnp.float32)
    partial_value = jnp.concatenate(
        [input_part.reshape(experts_here, 2, hidden_width, width), output_part[:, None]], axis=1
    )
    partial_half = partial_value.astype(jnp.bfloat16)
    terms = lax.optimization_barrier(partial_half).astype(jnp.float32)
    grad = lax.psum_scatter(
        terms.astype(jnp.bfloat16), "dp", scatter_dimension=3, tiled=True
    ).astype(jnp.float32)
    grad = lax.psum(grad.astype(jnp.bfloat16), "rep").astype(jnp.float32)
    squares = lax.psum(jnp.sum(grad * grad, axis=(2, 3)), "dp")
    current = (grad / (jnp.sqrt(squares) + norm_eps)[:, :, None, None]).astype(jnp.bfloat16)
    column_width = current.shape[3]
    scale = jnp.sqrt(jnp.float32(D))
    result = None
    n_dp = lax.axis_size("dp")
    matrices = experts_here * 3
    flat = current.reshape(matrices, hidden_width, column_width)
    padding = jnp.zeros((n_dp - matrices, hidden_width, column_width), jnp.bfloat16)
    outbound = jnp.concatenate([flat, padding], axis=0)
    owned = lax.all_to_all(outbound, "dp", split_axis=0, concat_axis=2, tiled=True)
    finished = whole_sweeps(owned[0], column_width, n_dp, ITERS, scale)
    returned = lax.all_to_all(finished[None], "dp", split_axis=2, concat_axis=0, tiled=True)
    result = returned[:matrices].reshape(experts_here, 3, hidden_width, column_width)
    return result


def solution(mesh):
    placed = (
        P(("dp", "rep"), None),
        P(("dp", "rep"), None),
        P(("dp", "rep"), None),
        P(("dp", "rep"), None),
        P(None, None, "dp"),
        P(("dp", "rep")),
        P(("dp", "rep")),
    )
    return jax.shard_map(
        per_device, mesh=mesh, in_specs=placed, out_specs=P(None, None, None, "dp"), check_vma=False
    )
```

profile of v0, /device:TPU:0, one launch (start us, length us, event | category | flops | bytes accessed | tf_op | source)
XLA Modules:
  0.0 795.3 jit_solution(15564926438498596758)
XLA Ops:
  6.5 0.0 copy-start
  6.5 0.0 all-gather.2.cloned.1.call-start
  6.5 0.7 all-gather.2.cloned.1.call-update
  7.3 0.0 reduce-scatter.2.cloned.1.call-start
  7.3 1.4 fusion.46
  8.7 2.5 fusion.34
  11.2 1.4 fusion.45
  12.6 2.5 select_select_fusion
  15.2 3.1 broadcast_select_fusion
  18.3 93.3 %all-gather.2.cloned.1.call-done = bf16[2,768,2048]{2,1,0:T(8,128)(2,1)} async-done(((bf16[2,768,256]{2,1,0:T(8,128)(2,1)}), bf16[2,768,2048]{2,1,0:T(8,128)(2,1)}) %all-gather.2.cloned.1.call-update) | async-done | bytes 6291472 | tf_op jit(solution)/shard_map/all_gather | solution.py:70
  111.6 7.8 fusion.15
  119.4 1.3 pad_maximum_fusion.1
  120.7 2.6 copy.31
  123.3 1.2 copy.32
  124.5 5.5 convert_bitcast_fusion
  129.9 0.0 copy-done
  130.0 0.0 copy-done.3
  130.0 6.9 convolution_convert_fusion
  136.9 10.4 %pad_maximum_fusion = bf16[2,3,768,2048]{3,2,1,0:T(8,128)(2,1)} fusion(bf16[2,1,768,2048]{3,2,1,0:T(8,128)(2,1)S(1)} %convert_bitcast_fusion, bf16[2,2,768,2048]{3,2,1,0:T(8,128)(2,1)S(1)} %bitcast.77), kind=kLoop, calls=%fused_computation | loop fusion | flops 9437184 | bytes 37748736 | tf_op jit(solution)/shard_map/concatenate | solution.py:83
  147.3 0.0 reduce-scatter.2.cloned.1.call-update
  147.4 0.0 all-reduce.3.cloned.1.call-start
  147.4 308.6 %reduce-scatter.2.cloned.1.call-done = bf16[2,3,768,256]{3,2,1,0:T(8,128)(2,1)} async-done(((bf16[2,3,768,2048]{3,2,1,0:T(8,128)(2,1)}), bf16[2,3,768,256]{3,2,1,0:T(8,128)(2,1)}) %reduce-scatter.2.cloned.1.call-update) | async-done | bytes 2359312 | tf_op jit(solution)/shard_map/reduce_scatter | solution.py:88
  456.1 0.0 all-reduce.3.cloned.1.call-update
  456.1 57.2 %all-reduce.3.cloned.1.call-done = bf16[2,3,768,256]{3,2,1,0:T(8,128)(2,1)} async-done(((bf16[2,3,768,256]{3,2,1,0:T(8,128)(2,1)}), bf16[2,3,768,256]{3,2,1,0:T(8,128)(2,1)}) %all-reduce.3.cloned.1.call-update) | async-done | bytes 2359312 | tf_op jit(solution)/shard_map/psum | solution.py:91
  513.2 2.5 fusion
  515.7 21.3 %psum.15 = f32[2,3]{1,0:T(2,128)S(1)} all-reduce(f32[2,3]{1,0:T(2,128)S(1)} %fusion), channel_id=1, replica_groups=mesh['dp'=8,'rep'=4] {'dp'}, use_global_device_ids=true, to_apply=%region_3.5 | all-reduce | flops 6 | bytes 48 | tf_op jit(solution)/shard_map/psum | solution.py:92
  537.0 0.0 copy-done.2
  537.0 0.9 fusion.1
  538.0 0.2 concatenate.18
  538.2 70.2 %all_to_all.30 = bf16[8,768,256]{2,1,0:T(8,128)(2,1)} all-to-all(bf16[8,768,256]{2,1,0:T(8,128)(2,1)S(1)} %concatenate.18), channel_id=1, replica_groups=mesh['dp'=8,'rep'=4] {'dp'}, dimensions={0} | all-to-all | bytes 6291456 | tf_op jit(solution)/shard_map/all_to_all | solution.py:102
  608.4 5.5 convolution_convert_fusion.2
  613.9 2.7 convert_reduce_fusion.1
  616.6 3.2 copy.34
  619.8 3.0 copy.35
  622.8 9.3 %add_convert_fusion = bf16[768,2048]{1,0:T(8,128)(2,1)} fusion(bf16[768,2048]{1,0:T(8,128)(2,1)} %copy.35, bf16[768,2048]{0,1:T(8,128)(2,1)S(1)} %bitcast.76, f32[768,768]{1,0:T(8,128)} %convert_reduce_fusion.1), kind=kOutput, calls=%fused_computation.7 | convolution fusion | flops 3331129344 | bytes 11796480 | tf_op jit(solution)/shard_map/dot_general | solution.py:38
  632.1 5.5 convolution_convert_fusion.1
  637.6 2.7 convert_reduce_fusion
  640.4 8.7 %fusion.8 = bf16[1,768,2048]{2,1,0:T(8,128)(2,1)S(1)} fusion(bf16[768,2048]{1,0:T(8,128)(2,1)} %add_convert_fusion, f32[768,768]{1,0:T(8,128)} %convert_reduce_fusion), kind=kOutput, calls=%fused_computation.19 | convolution fusion | flops 3332702208 | bytes 8650752 | tf_op jit(solution)/shard_map/dot_general | solution.py:38
  649.1 11.2 %copy.38 = bf16[1,768,2048]{1,0,2:T(2,128)(2,1)} copy(bf16[1,768,2048]{2,1,0:T(8,128)(2,1)S(1)} %fusion.8) | data formatting | bytes 6291456 | tf_op jit(solution)/shard_map/broadcast_in_dim | solution.py:104
  660.3 0.5 broadcast.198
  660.8 33.5 %reduce.3 = bf16[2048,768]{1,0:T(8,128)(2,1)} reduce(bf16[2048,1,768]{2,1,0:T(2,128)(2,1)} %bitcast.73, bf16[]{:T(256)} %broadcast.198), dimensions={1}, to_apply=%bitcast.67.reduce_sub_computation | reduce | bytes 6291458
  694.3 4.6 reshape.141
  699.0 72.8 %all_to_all.31 = bf16[8,2,98304]{2,1,0:T(2,128)(2,1)} all-to-all(bf16[8,2,98304]{2,1,0:T(2,128)(2,1)S(1)} %reshape.141), channel_id=1, replica_groups=mesh['dp'=8,'rep'=4] {'dp'}, dimensions={0} | all-to-all | bytes 6291456 | tf_op jit(solution)/shard_map/all_to_all | solution.py:104
  771.8 7.8 reshape.142
  779.6 3.3 copy.40
  782.9 0.0 copy-start.1
  782.9 1.6 slice.46
  784.5 4.3 copy.39
  (5 shorter events, 0.0 us)
Async XLA Ops:
  6.5 123.4 %copy-start = (bf16[512,2048]{1,0:T(8,128)(2,1)S(1)}, bf16[512,2048]{1,0:T(8,128)(2,1)}, u32[]{:S(2)}) copy-start(bf16[512,2048]{1,0:T(8,128)(2,1)} %param.13) | copy-start | bytes 6291460
  6.5 105.1 %all-gather.2.cloned.1.call-start = ((), (), s32[]{:S(2)}) async-start(), calls=%async_computation.3 | async-start | bytes 7077888 | tf_op jit(solution)/shard_map/all_gather | solution.py:70
  7.3 448.8 %reduce-scatter.2.cloned.1.call-start = ((), (), s32[]{:S(2)}) async-start(), calls=%async_computation.4 | async-start | bytes 21233664 | tf_op jit(solution)/shard_map/reduce_scatter | solution.py:88
  124.5 5.5 copy-start.3
  147.4 365.9 %all-reduce.3.cloned.1.call-start = ((), (), s32[]{:S(2)}) async-start(), calls=%async_computation.5 | async-start | bytes 4718592 | tf_op jit(solution)/shard_map/psum | solution.py:91
  513.2 23.8 %copy-start.2 = (bf16[2,3,768,256]{3,2,1,0:T(8,128)(2,1)S(1)}, bf16[2,3,768,256]{3,2,1,0:T(8,128)(2,1)}, u32[]{:S(2)}) copy-start(bf16[2,3,768,256]{3,2,1,0:T(8,128)(2,1)} %all-reduce.3.cloned.1.call-done) | copy-start | bytes 7077892
  782.9 5.9 copy-start.1
Sparse Core Ops, SparseCore 0:
  9.4 102.1 all-gather.1
  147.5 308.5 reduce-scatter.1
  458.4 54.7 all-reduce.2
where the time goes:
time: 796 us; the launch traced here: 795 us
  waiting for transfers between devices  460 us (58%)
  blocking collectives  164 us (21%)
  other arithmetic  62.2 us (8%)
  matrix products  49.3 us (6%)
  local copies, waits for them, and re-layouts  46.3 us (6%)
  between operations  13.2 us (2%)
    reduce_scatter x1, waiting for transfers between devices, per_device(): lax.psum_scatter(terms.astype(jnp.bfloat16), 'dp', scatter_dimension=3, t...  309 us
    all_gather x1, waiting for transfers between devices, per_device(): weights_all = lax.all_gather(down_weight, 'dp', axis=2, tiled=True)  93.3 us
    all_to_all x1, blocking collectives, per_device(): lax.all_to_all(finished[None], 'dp', split_axis=2, concat_axis=0, tiled=T...  72.8 us
    all_to_all x1, blocking collectives, per_device(): lax.all_to_all(outbound, 'dp', split_axis=0, concat_axis=2, tiled=True)  70.2 us
    psum x1, waiting for transfers between devices, per_device(): grad = lax.psum(grad.astype(jnp.bfloat16), 'rep').astype(jnp.float32)  57.2 us
    unnamed x1, other arithmetic  33.5 us
    psum x1, blocking collectives, per_device(): squares = lax.psum(jnp.sum(grad * grad, axis=(2, 3)), 'dp')  21.3 us
    dot_general x2, matrix products, whole_sweeps(): jnp.dot(poly, current, preferred_element_type=jnp.float32)  18 us
  transfers between devices with their start and end apart: 3, of which 3 were waited for; matrix products, arithmetic and copies ran while one was open for 1% of the time, Pallas kernels for 0%

commit v1 on v0

--- a/solution.py
+++ b/solution.py
@@ -101,7 +101,12 @@
     outbound = jnp.concatenate([flat, padding], axis=0)
     owned = lax.all_to_all(outbound, "dp", split_axis=0, concat_axis=2, tiled=True)
     finished = whole_sweeps(owned[0], column_width, n_dp, ITERS, scale)
-    returned = lax.all_to_all(finished[None], "dp", split_axis=2, concat_axis=0, tiled=True)
+    returned = jnp.concatenate(
+        lax.all_to_all(
+            jnp.stack(jnp.split(finished[None], lax.axis_size("dp"), axis=2)), "dp", 0, 0
+        ),
+        axis=0,
+    )
     result = returned[:matrices].reshape(experts_here, 3, hidden_width, column_width)
     return result
 

time: 796 us -> 733 us (0.921)
  other arithmetic: 62.2 us -> 28.6 us
  local copies, waits for them, and re-layouts: 46.3 us -> 16.8 us
    unnamed x1 -> x0, other arithmetic: 33.5 us -> none
    unnamed x12 -> x17, local copies, waits for them, and re-layouts: 16.2 us -> 0.39 us
    broadcast_in_dim x1 -> x0, local copies, waits for them, and re-layouts: 11.2 us -> none  [per_device(): finished[None]]
where the time goes in v1:
time: 733 us
  waiting for transfers between devices  460 us (63%)
  blocking collectives  164 us (22%)
  matrix products  50.3 us (7%)
  other arithmetic  28.6 us (4%)
  local copies, waits for them, and re-layouts  16.8 us (2%)
  between operations  13.3 us (2%)
    reduce_scatter x1, waiting for transfers between devices, per_device(): lax.psum_scatter(terms.astype(jnp.bfloat16), 'dp', scatter_dimension=3, t...  309 us
    all_gather x1, waiting for transfers between devices, per_device(): weights_all = lax.all_gather(down_weight, 'dp', axis=2, tiled=True)  93.3 us
    all_to_all x1, blocking collectives, per_device(): lax.all_to_all(jnp.stack(jnp.split(finished[None], lax.axis_size('dp'), a...  72.9 us
    all_to_all x1, blocking collectives, per_device(): lax.all_to_all(outbound, 'dp', split_axis=0, concat_axis=2, tiled=True)  69.4 us
    psum x1, waiting for transfers between devices, per_device(): grad = lax.psum(grad.astype(jnp.bfloat16), 'rep').astype(jnp.float32)  57.2 us
    psum x1, blocking collectives, per_device(): squares = lax.psum(jnp.sum(grad * grad, axis=(2, 3)), 'dp')  21.3 us
    dot_general x2, matrix products, whole_sweeps(): jnp.dot(poly, current, preferred_element_type=jnp.float32)  19 us
  transfers between devices with their start and end apart: 3, of which 3 were waited for; matrix products, arithmetic and copies ran while one was open for 1% of the time, Pallas kernels for 0%

profile of v1, /device:TPU:0, one launch (start us, length us, event | category | flops | bytes accessed | tf_op | source)
XLA Modules:
  0.0 732.6 jit_solution(7592095148430692616)
XLA Ops:
  6.5 0.0 copy-start
  6.5 0.0 all-gather.2.cloned.1.call-start
  6.5 0.7 all-gather.2.cloned.1.call-update
  7.3 0.0 reduce-scatter.2.cloned.1.call-start
  7.3 1.4 fusion.54
  8.7 2.5 fusion.42
  11.2 1.4 fusion.53
  12.6 2.5 select_select_fusion
  15.2 3.1 broadcast_select_fusion
  18.3 93.3 %all-gather.2.cloned.1.call-done = bf16[2,768,2048]{2,1,0:T(8,128)(2,1)} async-done(((bf16[2,768,256]{2,1,0:T(8,128)(2,1)}), bf16[2,768,2048]{2,1,0:T(8,128)(2,1)}) %all-gather.2.cloned.1.call-update) | async-done | bytes 6291472 | tf_op jit(solution)/shard_map/all_gather | solution.py:70
  111.6 7.8 %fusion.15 = (bf16[512,768]{1,0:T(8,128)(2,1)S(1)}, bf16[512,768]{1,0:T(8,128)(2,1)S(1)}, bf16[512,768]{1,0:T(8,128)(2,1)S(1)}) fusion(bf16[512,768]{1,0:T(8,128)(2,1)} %param.16, bf16[512,768]{1,0:T(8,128)(2,1)} %param.15, bf16[2,768,2048]{2,1,0:T(8,128)(2,1)} %all-gather.2.cloned.1.call-done, bf16[2,512]{1,0:T(2,128)(2,1)S(1)} %compare_convert_fusion, ...), kind=kOutput, calls=%fused_computation.35 | convolution fusion | flops 3230400512 | bytes 12322816 | tf_op jit(solution)/shard_map/erd,efd->rf/dot_general | solution.py:71
  119.4 1.3 pad_maximum_fusion.1
  120.7 2.6 copy.13
  123.3 1.2 copy.14
  124.5 5.5 convert_bitcast_fusion
  129.9 0.0 copy-done
  130.0 0.0 copy-done.4
  130.0 6.9 convolution_convert_fusion
  136.9 10.4 %pad_maximum_fusion = bf16[2,3,768,2048]{3,2,1,0:T(8,128)(2,1)} fusion(bf16[2,1,768,2048]{3,2,1,0:T(8,128)(2,1)S(1)} %convert_bitcast_fusion, bf16[2,2,768,2048]{3,2,1,0:T(8,128)(2,1)S(1)} %bitcast.102), kind=kLoop, calls=%fused_computation | loop fusion | flops 9437184 | bytes 37748736 | tf_op jit(solution)/shard_map/concatenate | solution.py:83
  147.3 0.0 reduce-scatter.2.cloned.1.call-update
  147.4 0.0 all-reduce.3.cloned.1.call-start
  147.4 308.6 %reduce-scatter.2.cloned.1.call-done = bf16[2,3,768,256]{3,2,1,0:T(8,128)(2,1)} async-done(((bf16[2,3,768,2048]{3,2,1,0:T(8,128)(2,1)}), bf16[2,3,768,256]{3,2,1,0:T(8,128)(2,1)}) %reduce-scatter.2.cloned.1.call-update) | async-done | bytes 2359312 | tf_op jit(solution)/shard_map/reduce_scatter | solution.py:88
  456.1 0.0 all-reduce.3.cloned.1.call-update
  456.1 57.2 %all-reduce.3.cloned.1.call-done = bf16[2,3,768,256]{3,2,1,0:T(8,128)(2,1)} async-done(((bf16[2,3,768,256]{3,2,1,0:T(8,128)(2,1)}), bf16[2,3,768,256]{3,2,1,0:T(8,128)(2,1)}) %all-reduce.3.cloned.1.call-update) | async-done | bytes 2359312 | tf_op jit(solution)/shard_map/psum | solution.py:91
  513.2 2.5 fusion
  515.7 21.3 %psum.15 = f32[2,3]{1,0:T(2,128)S(1)} all-reduce(f32[2,3]{1,0:T(2,128)S(1)} %fusion), channel_id=1, replica_groups=mesh['dp'=8,'rep'=4] {'dp'}, use_global_device_ids=true, to_apply=%region_3.5 | all-reduce | flops 6 | bytes 48 | tf_op jit(solution)/shard_map/psum | solution.py:92
  537.0 0.9 fusion.1
  538.0 0.2 concatenate.18
  538.2 69.4 %all_to_all.20 = bf16[8,768,256]{2,1,0:T(8,128)(2,1)S(1)} all-to-all(bf16[8,768,256]{2,1,0:T(8,128)(2,1)S(1)} %concatenate.18), channel_id=1, replica_groups=mesh['dp'=8,'rep'=4] {'dp'}, dimensions={0} | all-to-all | bytes 6291456 | tf_op jit(solution)/shard_map/all_to_all | solution.py:102
  607.7 3.2 copy.16
  610.9 4.8 copy.17
  615.6 5.6 convolution_convert_fusion.2
  621.2 2.7 convert_reduce_fusion.1
  623.9 10.3 %add_convert_fusion = bf16[768,2048]{1,0:T(8,128)(2,1)} fusion(bf16[768,2048]{1,0:T(8,128)(2,1)} %copy.17, bf16[768,2048]{0,1:T(8,128)(2,1)} %bitcast.101, f32[768,768]{1,0:T(8,128)} %convert_reduce_fusion.1), kind=kOutput, calls=%fused_computation.7 | convolution fusion | flops 3331129344 | bytes 11796480 | tf_op jit(solution)/shard_map/dot_general | solution.py:38
  634.2 5.5 convolution_convert_fusion.1
  639.7 2.7 convert_reduce_fusion
  642.4 8.7 %fusion.8 = bf16[1,768,2048]{2,1,0:T(8,128)(2,1)S(1)} fusion(bf16[768,2048]{1,0:T(8,128)(2,1)} %add_convert_fusion, f32[768,768]{1,0:T(8,128)} %convert_reduce_fusion), kind=kOutput, calls=%fused_computation.19 | convolution fusion | flops 3332702208 | bytes 8650752 | tf_op jit(solution)/shard_map/dot_general | solution.py:38
  651.2 0.1 fusion.41
  651.2 0.1 fusion.40
  651.3 0.1 fusion.39
  651.3 0.1 fusion.38
  651.4 0.1 fusion.37
  651.5 0.1 fusion.36
  651.5 0.1 fusion.35
  651.6 0.1 fusion.34
  651.7 0.0 copy-start.1
  651.7 72.9 %all_to_all.21 = bf16[8,1,768,256]{3,2,1,0:T(8,128)(2,1)S(1)} all-to-all(bf16[8,1,768,256]{3,2,1,0:T(8,128)(2,1)S(1)} %fusion.34), channel_id=1, replica_groups=mesh['dp'=8,'rep'=4] {'dp'}, dimensions={0} | all-to-all | bytes 6291456 | tf_op jit(solution)/shard_map/all_to_all | solution.py:105
  724.5 1.6 slice.46
  (8 shorter events, 0.0 us)
Async XLA Ops:
  6.5 123.4 %copy-start = (bf16[512,2048]{1,0:T(8,128)(2,1)S(1)}, bf16[512,2048]{1,0:T(8,128)(2,1)}, u32[]{:S(2)}) copy-start(bf16[512,2048]{1,0:T(8,128)(2,1)} %param.13) | copy-start | bytes 6291460
  6.5 105.1 %all-gather.2.cloned.1.call-start = ((), (), s32[]{:S(2)}) async-start(), calls=%async_computation.3 | async-start | bytes 7077888 | tf_op jit(solution)/shard_map/all_gather | solution.py:70
  7.3 448.8 %reduce-scatter.2.cloned.1.call-start = ((), (), s32[]{:S(2)}) async-start(), calls=%async_computation.4 | async-start | bytes 21233664 | tf_op jit(solution)/shard_map/reduce_scatter | solution.py:88
  124.5 5.5 copy-start.4
  147.4 365.9 %all-reduce.3.cloned.1.call-start = ((), (), s32[]{:S(2)}) async-start(), calls=%async_computation.5 | async-start | bytes 4718592 | tf_op jit(solution)/shard_map/psum | solution.py:91
  513.2 23.8 %copy-start.3 = (bf16[2,3,768,256]{3,2,1,0:T(8,128)(2,1)S(1)}, bf16[2,3,768,256]{3,2,1,0:T(8,128)(2,1)}, u32[]{:S(2)}) copy-start(bf16[2,3,768,256]{3,2,1,0:T(8,128)(2,1)} %all-reduce.3.cloned.1.call-done) | copy-start | bytes 7077892
  607.7 3.2 copy-start.2
  651.7 74.4 %copy-start.1 = (bf16[512,2048]{1,0:T(8,128)(2,1)S(1)}, bf16[512,2048]{1,0:T(8,128)(2,1)}, u32[]{:S(2)}) copy-start(bf16[512,2048]{1,0:T(8,128)(2,1)} %param.13) | copy-start | bytes 6291460
Sparse Core Ops, SparseCore 0:
  9.4 102.1 all-gather.1
  147.5 308.5 reduce-scatter.1
  458.4 54.7 all-reduce.2
